TPU v7x, 32 devices: a whole 2x2x4 slice. The times are simulated.
32 devices in a mesh: seq: 8 (over z, y), chan: 4 (over x, core).
Axes of the slice: x: 2, y: 2, z: 4, core: 2. Of those that a mesh axis runs over, the one named last changes fastest.
Arguments:
- hidden_in: bfloat16 [1024, 2048], P('seq', 'chan'), may hold values from -6 to 6
- norm_gain: float32 [2048], replicated, may hold values from 0.5 to 1.5
- in_weight: bfloat16 [2048, 2, 4096], P('seq', None, 'chan'), may hold values from -0.125 to 0.125
- conv_weight: float32 [2, 4, 4096], P(None, None, 'chan'), may hold values from -3 to 3
- conv_bias: float32 [2, 4096], P(None, 'chan'), may hold values from -0.5 to 0.5
- proj_weight: bfloat16 [2, 4096, 160], P(None, 'chan'), may hold values from -0.1875 to 0.1875
- step_weight: bfloat16 [2, 128, 4096], P(None, None, 'chan'), may hold values from -0.5 to 0.5
- decay_rate: float32 [2, 4096], P(None, 'chan'), may hold values from 0.00024414062 to 0.25
- skip_gain: float32 [2, 4096], P(None, 'chan'), may hold values from 0.5 to 1.5
- out_weight: bfloat16 [4096, 2048], P('chan', 'seq'), may hold values from -0.09375 to 0.09375
Outputs:
- mixed: bfloat16 [1024, 2048], P('seq', 'chan')
All inputs are finite; a program needn't handle non-finite values.
Results may differ from a plain program's by a relative error of at most 0.0095.
Values may be sent and summed in bfloat16 or wider, within the bound.
No kernel may reach another device: no remote copies, remote signals or barrier semaphores. Data moves between devices by JAX's collectives and lax.ppermute only.
A program may use at most 128 MiB of HBM per device.

v0:
```python
import jax
import jax.numpy as jnp
from jax import lax
from jax.sharding import PartitionSpec as P

STATE = 16
WIDTH = 4


def with_halo(block, sides, width):
    for axis, dim in sides:
        count = lax.axis_size(axis)
        forward = [(i, i + 1) for i in range(count - 1)]
        backward = [(target, source) for source, target in forward]
        low = lax.ppermute(
            lax.slice_in_dim(block, block.shape[dim] - width, None, axis=dim), axis, forward
        )
        high = lax.ppermute(lax.slice_in_dim(block, 0, width, axis=dim), axis, backward)
        block = jnp.concatenate([low, block, high], axis=dim)
    return block


def entering(array, axis, combine, identity, reverse):
    devices, here = (lax.axis_size(axis), lax.axis_index(axis))
    everything = jax.tree.map(lambda part: lax.all_gather(part, axis), array)
    start = jax.tree.map(
        lambda part, zero: jnp.broadcast_to(jnp.asarray(zero, part.dtype), part.shape),
        array,
        identity,
    )

    def hop(k, before):
        at = devices - 1 - k if reverse else k
        reached = at > here if reverse else at < here
        new = combine(before, jax.tree.map(lambda part: part[at], everything))
        return jax.tree.map(lambda a, b: jnp.where(reached, a, b), new, before)

    return lax.fori_loop(0, devices, hop, start)


def conv_taps(padded, conv_weight, conv_bias, length):
    reach = conv_weight.shape[1] - 1
    forward = jnp.zeros((length, padded.shape[1]), jnp.float32) + conv_bias[0][None, :]
    backward = jnp.zeros((length, padded.shape[1]), jnp.float32) + conv_bias[1][None, :]
    for offset in range(reach + 1):
        forward = forward + conv_weight[0, offset][None, :] * padded[offset : offset + length]
        begin = 2 * reach - offset
        backward = backward + conv_weight[1, offset][None, :] * padded[begin : begin + length]
    return jax.nn.silu(jnp.stack([forward, backward])).astype(jnp.bfloat16)


def sweep(drive_values, key_rows, query_rows, epsilon, initial, reverse, keeping):
    product = jnp.ones(initial.shape, jnp.float32)

    def advance(carry, current):
        product, state = carry
        drive_row, key_row, query_row, eps_row = current
        decay = 1.0 - eps_row[None, :] * (key_row * key_row)[:, None]
        state = decay * state + key_row[:, None] * (eps_row * drive_row)[None, :]
        product = decay * product
        if keeping == "reads":
            output = jnp.sum(query_row[:, None] * state, axis=0)
        else:
            output = None
        return ((product, state), output)

    (product, state), outputs = lax.scan(
        advance,
        (product, initial),
        (drive_values, key_rows, query_rows, epsilon),
        reverse=reverse,
        unroll=16,
    )
    return (product, state, outputs)


def combine(earlier, latter):
    return (latter[0] * earlier[0], latter[0] * earlier[1] + latter[1])


def per_device(
    hidden_in,
    norm_gain,
    in_weight,
    conv_weight,
    conv_bias,
    proj_weight,
    step_weight,
    decay_rate,
    skip_gain,
    out_weight,
):
    gathered = lax.all_gather(hidden_in, "chan", axis=1, tiled=True).astype(jnp.float32)
    normed = (
        gathered
        * lax.rsqrt(jnp.mean(gathered * gathered, axis=1, keepdims=True) + 1e-05)
        * norm_gain[None, :]
    ).astype(jnp.bfloat16)
    row_count = normed.shape[0]
    channels = in_weight.shape[2]
    piece = lax.all_gather(in_weight, "seq", axis=0, tiled=True)
    projected = jnp.dot(
        normed, piece.reshape(piece.shape[0], 2 * channels), preferred_element_type=jnp.float32
    )
    projected = projected.astype(jnp.bfloat16).reshape(row_count, 2, channels)
    branch = projected[:, 0, :]
    gate_half = projected[:, 1, :].astype(jnp.float32)
    padded = with_halo(branch, (("seq", 0),), WIDTH - 1).astype(jnp.float32)
    driven = conv_taps(padded, conv_weight, conv_bias, row_count)
    partial_value = jnp.einsum(
        "dte,def->tdf", driven, proj_weight, preferred_element_type=jnp.float32
    )
    features = lax.psum(partial_value, "chan")
    key_rows = features[:, :, :STATE]
    query_rows = features[:, :, STATE : 2 * STATE]
    low_rank = features[:, :, 2 * STATE :].astype(jnp.bfloat16)
    step_size = jnp.einsum(
        "tdr,dre->tde", low_rank, step_weight, preferred_element_type=jnp.float32
    )
    beta_rows = 2.0 * decay_rate[None, :, :] * jax.nn.sigmoid(step_size)
    epsilon = beta_rows / (1.0 + beta_rows * jnp.sum(key_rows * key_rows, axis=2, keepdims=True))
    drive_values = driven.astype(jnp.float32)
    zero_state = jnp.zeros((STATE, channels), jnp.float32)
    keeping = "summary"
    passes = [
        sweep(
            drive_values[direction],
            key_rows[:, direction],
            query_rows[:, direction],
            epsilon[:, direction],
            zero_state,
            direction == 1,
            keeping,
        )
        for direction in range(2)
    ]
    identity = (jnp.ones((STATE, channels), jnp.float32), zero_state)
    incoming_forward = entering((passes[0][0], passes[0][1]), "seq", combine, identity, False)[1]
    incoming_reverse = entering((passes[1][0], passes[1][1]), "seq", combine, identity, True)[1]
    incoming = [incoming_forward, incoming_reverse]
    total = jnp.zeros((row_count, channels), jnp.float32)
    for direction in range(2):
        reads = sweep(
            drive_values[direction],
            key_rows[:, direction],
            query_rows[:, direction],
            epsilon[:, direction],
            incoming[direction],
            direction == 1,
            "reads",
        )[2]
        total = total + reads + skip_gain[direction][None, :] * drive_values[direction]
    combined = (total * jax.nn.silu(gate_half)).astype(jnp.bfloat16)
    partial_out = jnp.dot(
        combined,
        lax.all_gather(out_weight, "seq", axis=1, tiled=True),
        preferred_element_type=jnp.float32,
    )
    summed = lax.psum(partial_out, "chan")
    share_width = summed.shape[1] // lax.axis_size("chan")
    share = lax.dynamic_slice_in_dim(summed, lax.axis_index("chan") * share_width, share_width, 1)
    return share.astype(jnp.bfloat16)


def solution(mesh):
    in_specs = (
        P("seq", "chan"),
        P(),
        P("seq", None, "chan"),
        P(None, None, "chan"),
        P(None, "chan"),
        P(None, "chan", None),
        P(None, None, "chan"),
        P(None, "chan"),
        P(None, "chan"),
        P("chan", "seq"),
    )
    out_specs = P("seq", "chan")
    return jax.shard_map(
        per_device, mesh=mesh, in_specs=in_specs, out_specs=out_specs, check_vma=False
    )
```

profile of v0, /device:TPU:0, one launch (start us, length us, event | category | flops | bytes accessed | tf_op | source)
XLA Modules:
  0.0 489.7 jit_solution(10717089666315897083)
XLA Ops:
  7.3 8.9 %all_gather.33 = bf16[128,2048]{1,0:T(8,128)(2,1)S(1)} all-gather(bf16[128,512]{1,0:T(8,128)(2,1)} %param.22), channel_id=1, replica_groups=mesh['seq'=8,'chan'=4] {'chan'}, dimensions={1}, use_global_device_ids=true | all-gather | bytes 655360 | tf_op jit(solution)/shard_map/all_gather | solution.py:93
  18.1 118.6 %all-gather.7.cloned.1.call-done = bf16[2048,2,1024]{2,1,0:T(2,128)(2,1)} async-done(((bf16[256,2,1024]{2,1,0:T(2,128)(2,1)}), bf16[2048,2,1024]{2,1,0:T(2,128)(2,1)}) %all-gather.7.cloned.1.call-update) | async-done | bytes 8388624 | tf_op jit(solution)/shard_map/all_gather | solution.py:101
  136.7 10.1 %copy.42 = bf16[256,8,2,1024]{3,1,2,0:T(8,128)(2,1)} copy(bf16[256,8,2,1024]{3,2,1,0:T(2,128)(2,1)} %bitcast.855) | data formatting | bytes 16777216
  146.8 4.7 convolution_convert_fusion
  152.0 1.3 collective-permute-start.1
  153.3 4.5 collective-permute-start
  157.8 1.5 fusion.335
  163.2 30.7 %all-reduce.3.cloned.1.call-done = f32[128,2,160]{0,2,1:T(8,128)} async-done(((f32[128,2,160]{0,2,1:T(8,128)}), f32[128,2,160]{0,2,1:T(8,128)}) %all-reduce.3.cloned.1.call-update) | async-done | bytes 163856 | tf_op jit(solution)/shard_map/psum | solution.py:113
  196.4 1.7 add_divide_fusion
  199.1 22.7 %while.92 = (s32[]{:T(128)}, f32[16,1024]{1,0:T(8,128)S(1)}, f32[16,1024]{1,0:T(8,128)S(1)}, f32[8,16,1024]{2,1,0:T(8,128)}, f32[8,16,16]{2,1,0:T(8,128)S(1)}, /...) while((s32[]{:T(128)}, f32[16,1024]{1,0:T(8,128)S(1)}, ...), condition=%wide.region_26.27_spmd.clone, body=%wide.region_25.26_spmd.clone.sunk | while | flops 2146579 | bytes 924200 | solution.py:67
  199.1 2.0 constant_dynamic-slice_fusion.231
  202.1 2.0 constant_dynamic-slice_fusion.231
  205.1 1.8 constant_dynamic-slice_fusion.231
  207.8 1.8 constant_dynamic-slice_fusion.231
  210.6 2.0 constant_dynamic-slice_fusion.231
  213.5 2.0 constant_dynamic-slice_fusion.231
  216.5 1.8 constant_dynamic-slice_fusion.231
  219.2 1.8 constant_dynamic-slice_fusion.231
  221.8 9.5 %while.90 = (s32[]{:T(128)}, f32[16,1024]{1,0:T(8,128)S(1)}, f32[16,1024]{1,0:T(8,128)S(1)}, f32[8,16,1024]{2,1,0:T(8,128)S(1)}, f32[8,16,16]{2,1,0:T(8,128)S(1)...) while((s32[]{:T(128)}, f32[16,1024]{1,0:T(8,128)S(1)}, ...), condition=%wide.region_4.5_spmd.clone, body=%wide.region_3.4_spmd.clone.sunk | while | flops 2146578 | bytes 924180 | solution.py:67
  231.3 37.0 %all-gather.1 = f32[128,1024]{1,0:T(8,128)} all-gather(f32[16,1024]{1,0:T(8,128)S(1)} %get-tuple-element.566), channel_id=3, replica_groups=mesh['seq'=8,'chan'=4] {'seq'}, dimensions={0}, use_global_device_ids=true | all-gather | bytes 589824 | tf_op jit(solution)/shard_map/all_gather | solution.py:25
  268.3 34.7 %all-gather.3 = f32[128,1024]{1,0:T(8,128)} all-gather(f32[16,1024]{1,0:T(8,128)S(1)} %get-tuple-element.570), channel_id=5, replica_groups=mesh['seq'=8,'chan'=4] {'seq'}, dimensions={0}, use_global_device_ids=true | all-gather | bytes 589824 | tf_op jit(solution)/shard_map/all_gather | solution.py:25
  303.0 33.4 %all-gather = f32[128,1024]{1,0:T(8,128)} all-gather(f32[16,1024]{1,0:T(8,128)S(1)} %get-tuple-element.565), channel_id=2, replica_groups=mesh['seq'=8,'chan'=4] {'seq'}, dimensions={0}, use_global_device_ids=true | all-gather | bytes 589824 | tf_op jit(solution)/shard_map/all_gather | solution.py:25
  336.4 7.5 %while.91 = (s32[]{:T(128)}, f32[16,1024]{1,0:T(8,128)S(1)}, s32[]{:T(128)}, f32[8,16,1024]{2,1,0:T(8,128)}, f32[8,16,1024]{2,1,0:T(8,128)}, /*index=5*/s32[]{:T(128)}, s32[]{:T(128)}) while((s32[]{:T(128)}, f32[16,1024]{1,0:T(8,128)S(1)}, s32[]{:T(128)}, f32[8,16,1024]{2,1,0:T(8,128)}, f32[8,16,1024]{2,1,0:T(8,128)}, ...), condition=%wide.region_6.7_spmd.clone, body=%wide.region_5.6_spmd.clone.sunk | while | flops 65540 | bytes 262253 | solution.py:38
  343.9 33.6 %all-gather.2 = f32[128,1024]{1,0:T(8,128)} all-gather(f32[16,1024]{1,0:T(8,128)S(1)} %get-tuple-element.569), channel_id=4, replica_groups=mesh['seq'=8,'chan'=4] {'seq'}, dimensions={0}, use_global_device_ids=true | all-gather | bytes 589824 | tf_op jit(solution)/shard_map/all_gather | solution.py:25
  377.5 7.5 %while.93 = (s32[]{:T(128)}, f32[16,1024]{1,0:T(8,128)S(1)}, s32[]{:T(128)}, f32[8,16,1024]{2,1,0:T(8,128)}, f32[8,16,1024]{2,1,0:T(8,128)}, /*index=5*/s32[]{:T(128)}, s32[]{:T(128)}, s32[]{:T(128)}, s32[]{:T(128)}) while((s32[]{:T(128)}, f32[16,1024]{1,0:T(8,128)S(1)}, s32[]{:T(128)}, f32[8,16,1024]{2,1,0:T(8,128)}, ...), condition=%wide.region_28.29_spmd.clone, body=%wide.region_27.28_spmd.clone.sunk | while | flops 65544 | bytes 262315 | solution.py:38
  385.9 33.0 %while.89 = (s32[]{:T(128)}, f32[16,1024]{1,0:T(8,128)S(1)}, f32[8,16,1024]{2,1,0:T(8,128)}, f32[8,16,1024]{2,1,0:T(8,128)}, f32[8,16,16]{2,1,0:T(8,128)S(1)}, /...) while((s32[]{:T(128)}, f32[16,1024]{1,0:T(8,128)S(1)}, ...), condition=%wide.region_46.47_spmd, body=%wide.region_29.46_spmd.sunk | while | flops 2408722 | bytes 2033121 | solution.py:67
  386.1 2.0 constant_dynamic-slice_fusion.229
  390.3 2.0 constant_dynamic-slice_fusion.229
  394.6 1.8 constant_dynamic-slice_fusion.229
  398.6 1.8 constant_dynamic-slice_fusion.229
  402.6 2.0 constant_dynamic-slice_fusion.229
  406.8 2.0 constant_dynamic-slice_fusion.229
  411.0 1.8 constant_dynamic-slice_fusion.229
  415.0 1.8 constant_dynamic-slice_fusion.229
  418.9 32.4 %while.88 = (s32[]{:T(128)}, f32[16,1024]{1,0:T(8,128)S(1)}, f32[8,16,1024]{2,1,0:T(8,128)S(1)}, f32[8,16,1024]{2,1,0:T(8,128)S(1)}, f32[8,16,16]{2,1,0:T(8,128)...) while((s32[]{:T(128)}, f32[16,1024]{1,0:T(8,128)S(1)}, ...), condition=%wide.region_24.25_spmd, body=%wide.region_7.24_spmd.sunk | while | flops 2490641 | bytes 2106965 | solution.py:67
  420.0 1.1 fusion.360
  424.0 1.1 fusion.360
  428.0 1.1 fusion.360
  431.0 1.1 fusion.359
  432.1 1.1 fusion.360
  436.1 1.1 fusion.360
  440.2 1.1 fusion.360
  444.2 1.1 fusion.360
  447.2 1.1 fusion.359
  448.3 1.1 fusion.360
  451.3 1.5 fusion.203
  452.8 2.9 fusion.342
  455.7 26.7 %all-reduce.4 = bf16[128,2048]{1,0:T(8,128)(2,1)S(1)} all-reduce(f32[128,2048]{1,0:T(8,128)S(1)} %fusion.342), channel_id=1, replica_groups=mesh['seq'=8,'chan'=4] {'chan'}, use_global_device_ids=true, to_apply=%region_47.48 | all-reduce | flops 262144 | bytes 1572864 | tf_op jit(solution)/shard_map/psum | solution.py:159
  (837 shorter events, 76.6 us)
Async XLA Ops:
  6.5 153.8 %copy-start = (bf16[2,1024,160]{1,2,0:T(8,128)(2,1)S(1)}, bf16[2,1024,160]{1,2,0:T(8,128)(2,1)}, u32[]{:S(2)}) copy-start(bf16[2,1024,160]{1,2,0:T(8,128)(2,1)} %param.27) | copy-start | bytes 1966084
  6.5 130.2 %all-gather.7.cloned.1.call-start = ((), (), s32[]{:S(2)}) async-start(), calls=%async_computation | async-start | bytes 9437184 | tf_op jit(solution)/shard_map/all_gather | solution.py:101
  7.3 186.6 %all-reduce.3.cloned.1.call-start = ((), (), s32[]{:S(2)}) async-start(), calls=%async_computation.1 | async-start | bytes 327680 | tf_op jit(solution)/shard_map/psum | solution.py:113
  136.7 10.1 %copy-start.4 = (f32[2048]{0:T(1024)S(1)}, f32[2048]{0:T(1024)}, u32[]{:S(2)}) copy-start(f32[2048]{0:T(1024)} %param.23) | copy-start | bytes 24580
  151.5 10.6 %copy-start.5 = (f32[2,1024]{1,0:T(2,128)S(1)}, f32[2,1024]{1,0:T(2,128)}, u32[]{:S(2)}) copy-start(f32[2,1024]{1,0:T(2,128)} %param.29) | copy-start | bytes 24580
  151.5 10.7 %copy-start.6 = (f32[2,1024]{1,0:T(2,128)S(1)}, f32[2,1024]{1,0:T(2,128)}, u32[]{:S(2)}) copy-start(f32[2,1024]{1,0:T(2,128)} %param.30) | copy-start | bytes 24580
  152.0 7.5 %collective-permute-start.1 = (bf16[3,1024]{1,0:T(4,128)(2,1)S(1)}, bf16[3,1024]{1,0:T(4,128)(2,1)S(1)}, u32[]{:S(2)}, u32[]{:S(2)}) collective-permute-start(bf16[3,1024]{1,0:T(4,128)(2,1)S(1)} %bitcast.1151), channel_id=1, source_target_pairs={{4,0},{8,4},{12,8},{16,12},{20,16},{24,20},{28,24},{5,1},{9,5},{13... | collective-permute-start | bytes 18440 | tf_op jit(solution)/shard_map/ppermute | solution.py:18
  153.3 6.2 %collective-permute-start = (bf16[3,1024]{1,0:T(4,128)(2,1)S(1)}, bf16[3,1024]{1,0:T(4,128)(2,1)S(1)}, u32[]{:S(2)}, u32[]{:S(2)}) collective-permute-start(bf16[3,1024]{1,0:T(4,128)(2,1)S(1)} %bitcast.1150), channel_id=1, source_target_pairs={{0,4},{4,8},{8,12},{12,16},{16,20},{20,24},{24,28},{1,5},{5,9},{9,... | collective-permute-start | bytes 18440 | tf_op jit(solution)/shard_map/ppermute | solution.py:15
  161.4 291.4 %all-gather.9.cloned.1.call-start = ((), (), s32[]{:S(2)}) async-start(), calls=%async_computation.2 | async-start | bytes 4718592 | tf_op jit(solution)/shard_map/all_gather | solution.py:156
  163.2 35.9 %copy-start.1 = (f32[16,1024]{1,0:T(8,128)S(1)}, f32[16,1024]{1,0:T(8,128)}, u32[]{:S(2)}) copy-start(f32[16,1024]{1,0:T(8,128)} %custom-call.4) | copy-start | bytes 196612
  163.2 35.9 %copy-start.2 = (f32[16,1024]{1,0:T(8,128)S(1)}, f32[16,1024]{1,0:T(8,128)}, u32[]{:S(2)}) copy-start(f32[16,1024]{1,0:T(8,128)} %custom-call.3) | copy-start | bytes 196612
  231.3 154.6 %copy-start.3 = (f32[8,16,16]{2,1,0:T(8,128)}, f32[8,16,16]{2,1,0:T(8,128)S(1)}, u32[]{:S(2)}) copy-start(f32[8,16,16]{2,1,0:T(8,128)S(1)} %get-tuple-element.2563) | copy-start | bytes 24580
Sparse Core Ops, SparseCore 0:
  9.5 127.1 all-gather.6
  161.5 32.3 all-reduce.2
  195.9 86.4 all-gather.8
where the time goes:
time: 494 us; the launch traced here: 490 us
  blocking collectives  174 us (35%)
  waiting for transfers between devices  151 us (31%)
  local copies, waits for them, and re-layouts  69.2 us (14%)
  other arithmetic  59.8 us (12%)
  between operations  13.4 us (3%)
  matrix products  10.3 us (2%)
  loops' own time  6.06 us (1%)
  starting transfers between devices  5.92 us (1%)
    all_gather x4, blocking collectives, entering(): everything = jax.tree.map(lambda part: lax.all_gather(part, axis), array)  139 us
    all_gather x1, waiting for transfers between devices, per_device(): piece = lax.all_gather(in_weight, 'seq', axis=0, tiled=True)  119 us
    slice x32, local copies, waits for them, and re-layouts, sweep(): lax.scan(advance, (product, initial), (drive_values, key_rows, query_rows...  34.3 us
    psum x1, waiting for transfers between devices, per_device(): features = lax.psum(partial_value, 'chan')  30.7 us
    psum x1, blocking collectives, per_device(): summed = lax.psum(partial_out, 'chan')  26.7 us
    reduce_sum x136, other arithmetic, advance(): output = jnp.sum(query_row[:, None] * state, axis=0)  17.7 us
    select_n x16, other arithmetic, hop(): return jax.tree.map(lambda a, b: jnp.where(reached, a, b), new, before)  14.6 us
    mul x32, other arithmetic, advance(): decay = 1.0 - eps_row[None, :] * (key_row * key_row)[:, None]  12.7 us
  transfers between devices with their start and end apart: 5, of which 2 were waited for; matrix products, arithmetic and copies ran while one was open for 24% of the time, Pallas kernels for 0%

commit v1 on v0

--- a/solution.py
+++ b/solution.py
@@ -110,7 +110,7 @@
     partial_value = jnp.einsum(
         "dte,def->tdf", driven, proj_weight, preferred_element_type=jnp.float32
     )
-    features = lax.psum(partial_value, "chan")
+    features = jnp.sum(lax.all_gather(partial_value, "chan"), axis=0)
     key_rows = features[:, :, :STATE]
     query_rows = features[:, :, STATE : 2 * STATE]
     low_rank = features[:, :, 2 * STATE :].astype(jnp.bfloat16)

time: 494 us -> 507 us (1.026)
  other arithmetic: 59.8 us -> 97.6 us
  waiting for transfers between devices: 151 us -> 118 us
    psum x1 -> x0, waiting for transfers between devices: 30.7 us -> none  [per_device(): features = lax.psum(partial_value, 'chan')]
    mul x32, other arithmetic: 12.7 us -> 27.3 us  [advance(): decay = 1.0 - eps_row[None, :] * (key_row * key_row)[:, None]]
    add x16, other arithmetic: 5.87 us -> 16.8 us  [advance(): state = decay * state + key_row[:, None] * (eps_row * drive_row)[None, :]]
    mul x16, other arithmetic: 3.1 us -> 13.8 us  [advance(): product = decay * product]
    mul x16, local copies, waits for them, and re-layouts: 8.66 us -> 16.8 us  [advance(): output = jnp.sum(query_row[:, None] * state, axis=0)]
    all_gather x0 -> x1, blocking collectives: none -> 8.1 us  [per_device(): features = jnp.sum(lax.all_gather(partial_value, 'chan'), axis=0)]
  transfers between devices with their start and end apart: 5 -> 4, of which waited for: 2 -> 1; matrix products, arithmetic and copies ran while one was open for 24% -> 35% of each run, Pallas kernels for 0% -> 0%
where the time goes in v1:
time: 507 us; the launch traced here: 501 us
  blocking collectives  177 us (35%)
  waiting for transfers between devices  118 us (23%)
  other arithmetic  97.6 us (19%)
  local copies, waits for them, and re-layouts  73.7 us (15%)
  between operations  13.7 us (3%)
  matrix products  9.63 us (2%)
  loops' own time  5.97 us (1%)
  starting transfers between devices  5.88 us (1%)
    all_gather x4, blocking collectives, entering(): everything = jax.tree.map(lambda part: lax.all_gather(part, axis), array)  135 us
    all_gather x1, waiting for transfers between devices, per_device(): piece = lax.all_gather(in_weight, 'seq', axis=0, tiled=True)  116 us
    slice x32, local copies, waits for them, and re-layouts, sweep(): lax.scan(advance, (product, initial), (drive_values, key_rows, query_rows...  33.4 us
    mul x32, other arithmetic, advance(): decay = 1.0 - eps_row[None, :] * (key_row * key_row)[:, None]  27.3 us
    psum x1, blocking collectives, per_device(): summed = lax.psum(partial_out, 'chan')  25.5 us
    reduce_sum x136, other arithmetic, advance(): output = jnp.sum(query_row[:, None] * state, axis=0)  17.7 us
    mul x16, local copies, waits for them, and re-layouts, advance(): output = jnp.sum(query_row[:, None] * state, axis=0)  16.8 us
    add x16, other arithmetic, advance(): state = decay * state + key_row[:, None] * (eps_row * drive_row)[None, :]  16.8 us
  transfers between devices with their start and end apart: 4, of which 1 were waited for; matrix products, arithmetic and copies ran while one was open for 35% of the time, Pallas kernels for 0%

profile of v1, /device:TPU:0, one launch (start us, length us, event | category | flops | bytes accessed | tf_op | source)
XLA Modules:
  0.0 501.2 jit_solution(18373733635236604662)
XLA Ops:
  11.3 8.9 %all_gather.39 = bf16[128,2048]{1,0:T(8,128)(2,1)S(1)} all-gather(bf16[128,512]{1,0:T(8,128)(2,1)} %param.22), channel_id=1, replica_groups=mesh['seq'=8,'chan'=4] {'chan'}, dimensions={1}, use_global_device_ids=true | all-gather | bytes 655360 | tf_op jit(solution)/shard_map/all_gather | solution.py:93
  20.3 116.3 %all-gather.8.cloned.1.call-done = bf16[2048,2,1024]{2,1,0:T(2,128)(2,1)} async-done(((bf16[256,2,1024]{2,1,0:T(2,128)(2,1)}), bf16[2048,2,1024]{2,1,0:T(2,128)(2,1)}) %all-gather.8.cloned.1.call-update) | async-done | bytes 8388624 | tf_op jit(solution)/shard_map/all_gather | solution.py:101
  136.7 10.1 %copy.46 = bf16[256,8,2,1024]{3,1,2,0:T(8,128)(2,1)} copy(bf16[256,8,2,1024]{3,2,1,0:T(2,128)(2,1)} %bitcast.857) | data formatting | bytes 16777216
  146.8 4.7 convolution_convert_fusion
  153.3 4.5 collective-permute-start
  160.7 8.1 %all-gather = f32[512,2,160]{0,2,1:T(8,128)S(1)} all-gather(f32[128,2,160]{0,2,1:T(8,128)S(1)} %convolution_bitcast_fusion), channel_id=2, replica_groups=mesh['seq'=8,'chan'=4] {'chan'}, dimensions={0}, use_global_device_ids=true | all-gather | bytes 819200 | tf_op jit(solution)/shard_map/all_gather | solution.py:113
  174.5 1.7 add_divide_fusion
  177.1 50.6 %while.92 = (s32[]{:T(128)}, f32[16,1024]{1,0:T(8,128)}, f32[16,1024]{1,0:T(8,128)}, f32[8,16,1024]{2,1,0:T(8,128)}, f32[8,16,16]{2,1,0:T(8,128)}, /*index=5*/f3...) while((s32[]{:T(128)}, f32[16,1024]{1,0:T(8,128)}, ...), condition=%wide.region_26.27_spmd.clone, body=%wide.region_25.26_spmd.clone.sunk | while | flops 2146579 | bytes 924200 | solution.py:67
  178.3 2.0 constant_dynamic-slice_fusion.231
  183.3 1.7 constant_dynamic-slice_fusion.231
  185.2 1.8 multiply_add_fusion.53
  187.1 1.6 fusion.367
  189.7 2.0 constant_dynamic-slice_fusion.231
  191.9 1.8 multiply_add_fusion.53
  193.7 1.6 fusion.367
  196.3 1.7 constant_dynamic-slice_fusion.231
  198.3 1.8 multiply_add_fusion.53
  200.1 1.6 fusion.367
  202.7 1.8 constant_dynamic-slice_fusion.231
  204.7 1.8 multiply_add_fusion.53
  206.6 1.6 fusion.367
  209.2 2.0 constant_dynamic-slice_fusion.231
  211.4 1.8 multiply_add_fusion.53
  215.9 1.8 constant_dynamic-slice_fusion.231
  217.8 1.8 multiply_add_fusion.53
  219.7 1.6 fusion.367
  222.3 1.8 constant_dynamic-slice_fusion.231
  224.3 1.8 multiply_add_fusion.53
  226.1 1.6 fusion.367
  227.8 9.6 %while.90 = (s32[]{:T(128)}, f32[16,1024]{1,0:T(8,128)S(1)}, f32[16,1024]{1,0:T(8,128)S(1)}, f32[8,16,1024]{2,1,0:T(8,128)S(1)}, f32[8,16,16]{2,1,0:T(8,128)S(1)...) while((s32[]{:T(128)}, f32[16,1024]{1,0:T(8,128)S(1)}, ...), condition=%wide.region_4.5_spmd.clone, body=%wide.region_3.4_spmd.clone.sunk | while | flops 2146578 | bytes 924180 | solution.py:67
  237.3 34.4 %all-gather.2 = f32[128,1024]{1,0:T(8,128)} all-gather(f32[16,1024]{1,0:T(8,128)S(1)} %get-tuple-element.566), channel_id=4, replica_groups=mesh['seq'=8,'chan'=4] {'seq'}, dimensions={0}, use_global_device_ids=true | all-gather | bytes 589824 | tf_op jit(solution)/shard_map/all_gather | solution.py:25
  271.8 33.5 %all-gather.4 = f32[128,1024]{1,0:T(8,128)} all-gather(f32[16,1024]{1,0:T(8,128)} %get-tuple-element.570), channel_id=6, replica_groups=mesh['seq'=8,'chan'=4] {'seq'}, dimensions={0}, use_global_device_ids=true | all-gather | bytes 589824 | tf_op jit(solution)/shard_map/all_gather | solution.py:25
  305.3 33.3 %all-gather.1 = f32[128,1024]{1,0:T(8,128)} all-gather(f32[16,1024]{1,0:T(8,128)S(1)} %get-tuple-element.565), channel_id=3, replica_groups=mesh['seq'=8,'chan'=4] {'seq'}, dimensions={0}, use_global_device_ids=true | all-gather | bytes 589824 | tf_op jit(solution)/shard_map/all_gather | solution.py:25
  338.6 7.5 %while.91 = (s32[]{:T(128)}, f32[16,1024]{1,0:T(8,128)S(1)}, s32[]{:T(128)}, f32[8,16,1024]{2,1,0:T(8,128)}, f32[8,16,1024]{2,1,0:T(8,128)}, /*index=5*/s32[]{:T(128)}, s32[]{:T(128)}) while((s32[]{:T(128)}, f32[16,1024]{1,0:T(8,128)S(1)}, s32[]{:T(128)}, f32[8,16,1024]{2,1,0:T(8,128)}, f32[8,16,1024]{2,1,0:T(8,128)}, ...), condition=%wide.region_6.7_spmd.clone, body=%wide.region_5.6_spmd.clone.sunk | while | flops 65540 | bytes 262253 | solution.py:38
  346.1 33.2 %all-gather.3 = f32[128,1024]{1,0:T(8,128)} all-gather(f32[16,1024]{1,0:T(8,128)S(1)} %copy-done.3), channel_id=5, replica_groups=mesh['seq'=8,'chan'=4] {'seq'}, dimensions={0}, use_global_device_ids=true | all-gather | bytes 589824 | tf_op jit(solution)/shard_map/all_gather | solution.py:25
  379.3 7.5 %while.93 = (s32[]{:T(128)}, f32[16,1024]{1,0:T(8,128)S(1)}, s32[]{:T(128)}, f32[8,16,1024]{2,1,0:T(8,128)}, f32[8,16,1024]{2,1,0:T(8,128)}, /*index=5*/s32[]{:T(128)}, s32[]{:T(128)}, s32[]{:T(128)}, s32[]{:T(128)}) while((s32[]{:T(128)}, f32[16,1024]{1,0:T(8,128)S(1)}, s32[]{:T(128)}, f32[8,16,1024]{2,1,0:T(8,128)}, ...), condition=%wide.region_28.29_spmd.clone, body=%wide.region_27.28_spmd.clone.sunk | while | flops 65544 | bytes 262315 | solution.py:38
  386.9 43.7 %while.89 = (s32[]{:T(128)}, f32[16,1024]{1,0:T(8,128)S(1)}, f32[8,16,1024]{2,1,0:T(8,128)S(1)}, f32[8,16,1024]{2,1,0:T(8,128)}, f32[8,16,16]{2,1,0:T(8,128)}, /...) while((s32[]{:T(128)}, f32[16,1024]{1,0:T(8,128)S(1)}, ...), condition=%wide.region_46.47_spmd, body=%wide.region_29.46_spmd.sunk | while | flops 2408722 | bytes 2033121 | solution.py:67
  389.3 2.0 constant_dynamic-slice_fusion.229
  394.8 1.7 constant_dynamic-slice_fusion.229
  400.2 2.0 constant_dynamic-slice_fusion.229
  405.7 1.7 constant_dynamic-slice_fusion.229
  411.0 1.8 constant_dynamic-slice_fusion.229
  416.4 2.0 constant_dynamic-slice_fusion.229
  422.0 1.8 constant_dynamic-slice_fusion.229
  427.4 1.8 constant_dynamic-slice_fusion.229
  431.4 32.3 %while.88 = (s32[]{:T(128)}, f32[16,1024]{1,0:T(8,128)S(1)}, f32[8,16,1024]{2,1,0:T(8,128)S(1)}, f32[8,16,1024]{2,1,0:T(8,128)S(1)}, f32[8,16,16]{2,1,0:T(8,128)...) while((s32[]{:T(128)}, f32[16,1024]{1,0:T(8,128)S(1)}, ...), condition=%wide.region_24.25_spmd, body=%wide.region_7.24_spmd.sunk | while | flops 2490641 | bytes 2106965 | solution.py:67
  465.3 2.9 fusion.342
  468.2 25.5 %all-reduce.1 = bf16[128,2048]{1,0:T(8,128)(2,1)S(1)} all-reduce(f32[128,2048]{1,0:T(8,128)S(1)} %fusion.342), channel_id=1, replica_groups=mesh['seq'=8,'chan'=4] {'chan'}, use_global_device_ids=true, to_apply=%region_47.48 | all-reduce | flops 262144 | bytes 1572864 | tf_op jit(solution)/shard_map/psum | solution.py:159
  (837 shorter events, 112.0 us)
Async XLA Ops:
  6.5 153.8 %copy-start = (bf16[2,1024,160]{1,2,0:T(8,128)(2,1)S(1)}, bf16[2,1024,160]{1,2,0:T(8,128)(2,1)}, u32[]{:S(2)}) copy-start(bf16[2,1024,160]{1,2,0:T(8,128)(2,1)} %param.27) | copy-start | bytes 1966084
  6.5 130.2 %all-gather.8.cloned.1.call-start = ((), (), s32[]{:S(2)}) async-start(), calls=%async_computation | async-start | bytes 9437184 | tf_op jit(solution)/shard_map/all_gather | solution.py:101
  7.3 458.0 %all-gather.10.cloned.1.call-start = ((), (), s32[]{:S(2)}) async-start(), calls=%async_computation.1 | async-start | bytes 4718592 | tf_op jit(solution)/shard_map/all_gather | solution.py:156
  136.7 10.1 %copy-start.6 = (f32[2048]{0:T(1024)S(1)}, f32[2048]{0:T(1024)}, u32[]{:S(2)}) copy-start(f32[2048]{0:T(1024)} %param.23) | copy-start | bytes 24580
  152.0 7.5 %collective-permute-start.1 = (bf16[3,1024]{1,0:T(4,128)(2,1)S(1)}, bf16[3,1024]{1,0:T(4,128)(2,1)S(1)}, u32[]{:S(2)}, u32[]{:S(2)}) collective-permute-start(bf16[3,1024]{1,0:T(4,128)(2,1)S(1)} %bitcast.1151), channel_id=1, source_target_pairs={{4,0},{8,4},{12,8},{16,12},{20,16},{24,20},{28,24},{5,1},{9,5},{13... | collective-permute-start | bytes 18440 | tf_op jit(solution)/shard_map/ppermute | solution.py:18
  153.3 6.2 %collective-permute-start = (bf16[3,1024]{1,0:T(4,128)(2,1)S(1)}, bf16[3,1024]{1,0:T(4,128)(2,1)S(1)}, u32[]{:S(2)}, u32[]{:S(2)}) collective-permute-start(bf16[3,1024]{1,0:T(4,128)(2,1)S(1)} %bitcast.1150), channel_id=1, source_target_pairs={{0,4},{4,8},{8,12},{12,16},{16,20},{20,24},{24,28},{1,5},{5,9},{9,... | collective-permute-start | bytes 18440 | tf_op jit(solution)/shard_map/ppermute | solution.py:15
  174.5 53.3 %copy-start.1 = (f32[16,1024]{1,0:T(8,128)S(1)}, f32[16,1024]{1,0:T(8,128)}, u32[]{:S(2)}) copy-start(f32[16,1024]{1,0:T(8,128)} %custom-call.1) | copy-start | bytes 196612
  174.5 53.3 %copy-start.2 = (f32[16,1024]{1,0:T(8,128)S(1)}, f32[16,1024]{1,0:T(8,128)}, u32[]{:S(2)}) copy-start(f32[16,1024]{1,0:T(8,128)} %custom-call) | copy-start | bytes 196612
  227.7 118.4 %copy-start.3 = (f32[16,1024]{1,0:T(8,128)S(1)}, f32[16,1024]{1,0:T(8,128)}, u32[]{:S(2)}) copy-start(f32[16,1024]{1,0:T(8,128)} %get-tuple-element.569) | copy-start | bytes 196612
  237.3 149.5 %copy-start.5 = (f32[8,16,16]{2,1,0:T(8,128)}, f32[8,16,16]{2,1,0:T(8,128)S(1)}, u32[]{:S(2)}) copy-start(f32[8,16,16]{2,1,0:T(8,128)S(1)} %get-tuple-element.2560) | copy-start | bytes 24580
  430.6 0.8 copy-start.4
Sparse Core Ops, SparseCore 0:
  9.5 127.1 all-gather.7
  138.7 72.8 all-gather.9
